TPU v7x, 32 devices: a whole 2x2x4 slice. The times are simulated.
32 devices in a mesh: tm: 8 (over y, x, core), sr: 4 (over z).
Axes of the slice: x: 2, y: 2, z: 4, core: 2. Of those that a mesh axis runs over, the one named last changes fastest.
Arguments:
- observations: bfloat16 [1024, 65536], P(None, ('sr', 'tm')), may hold values from -6 to 6
- loadings: float32 [65536, 128], P(('sr', 'tm')), may hold values from -0.0007324219 to 0.0007324219
- noise_precision: float32 [65536], P(('sr', 'tm')), may hold values from 0.5 to 4
- transition: float32 [128, 128], replicated, may hold values from -1 to 1, as said below
- filter_cov: float32 [128, 128], replicated, may hold values from -1 to 1, as said below
- smoother_gain: float32 [128, 128], replicated, may hold values from -1 to 1, as said below
- smoothed_cov: float32 [128, 128], replicated, may hold values from -1 to 1, as said below
Outputs:
- smoothed_factors: float32 [1024, 128], P('tm')
- new_loadings: float32 [65536, 128], P(('sr', 'tm'))
- new_transition: float32 [128, 128], replicated
Inputs may be any that keep to these rules, and one draw needn't show every extreme that they name: `transition`: the spectral radius is below one. `filter_cov`: symmetric positive definite. `smoother_gain`: the spectral radius is below one. `smoothed_cov`: symmetric positive definite.
All inputs are finite; a program needn't handle non-finite values.
Results may differ from a plain program's by a relative error of at most 0.00175.
The roundings to bfloat16 on the way count: a program that leaves them out, or rounds other values in their place, can miss the bound.
Values may be sent and summed in bfloat16 or wider, within the bound.
A program may use at most 64 MiB of HBM per device.

v0:
```python
import jax
import jax.numpy as jnp
from jax import lax
from jax.sharding import PartitionSpec as P

precise = lax.Precision.HIGHEST


def carried_in(part, axis, combine, identity, reverse):
    count = lax.axis_size(axis)
    place = lax.axis_index(axis)
    ahead = count - 1 - place if reverse else place
    gathered = jax.tree.map(lambda a: lax.all_gather(a, axis), part)
    state = jax.tree.map(lambda a, e: jnp.zeros_like(a) + jnp.asarray(e, a.dtype), part, identity)

    def one(hop, state):
        source = count - 1 - hop if reverse else hop
        return combine(
            state, jax.tree.map(lambda a: lax.dynamic_index_in_dim(a, source, 0, False), gathered)
        )

    return lax.fori_loop(0, ahead, one, state)


def shifted(value, axis, steps):
    count = lax.axis_size(axis)
    leading, last = (max(0, -steps), min(count, count - steps))
    return lax.ppermute(value, axis, [(source, source + steps) for source in range(leading, last)])


def dot_high(left, right):
    return jnp.dot(left, right, precision=precise, preferred_element_type=jnp.float32)


def matrix_power(matrix, exponent):
    result = jnp.eye(matrix.shape[0], dtype=jnp.float32)
    square = matrix
    remain = exponent
    while remain > 0:
        if remain % 2 == 1:
            result = dot_high(result, square)
        remain = remain // 2
        if remain > 0:
            square = dot_high(square, square)
    return result


def block_prefix(inputs, matrix):
    length = inputs.shape[0]
    width = inputs.shape[1]
    totals = inputs
    raised = matrix
    offset = 1
    while offset < length:
        moved = jnp.concatenate(
            [jnp.zeros((offset, width), jnp.float32), totals[: length - offset]], axis=0
        )
        totals = totals + dot_high(moved, raised.T)
        offset = offset * 2
        if offset < length:
            raised = dot_high(raised, raised)
    return totals


def propagate(start, matrix, length):
    carried = dot_high(matrix, start)[None, :]
    raised = matrix
    while carried.shape[0] < length:
        carried = jnp.concatenate([carried, dot_high(carried, raised.T)], axis=0)
        raised = dot_high(raised, raised)
    return carried


def compose(earlier, later):
    return (dot_high(later[0], earlier[0]), dot_high(later[0], earlier[1]) + later[1])


def local(
    observations, loadings, noise_precision, transition, filter_cov, smoother_gain, smoothed_cov
):
    blocks = lax.axis_size("tm")
    position = lax.axis_index("tm")
    width = transition.shape[0]
    steps_dev = observations.shape[0] // blocks
    scaled = (noise_precision[:, None] * loadings).astype(jnp.bfloat16)
    window = observations
    partial_value = lax.psum_scatter(
        jnp.dot(window, scaled, preferred_element_type=jnp.float32),
        "tm",
        scatter_dimension=0,
        tiled=True,
    )
    info_part = dot_high(loadings.T, noise_precision[:, None] * loadings)
    proj = lax.psum(partial_value, "sr")
    info = lax.psum(info_part, ("tm", "sr"))
    closed = transition - dot_high(filter_cov, dot_high(info, transition))
    inputs = dot_high(proj, filter_cov.T)
    local_filter = block_prefix(inputs, closed)
    whole_filter = matrix_power(closed, steps_dev)
    identity_pair = (jnp.eye(width, dtype=jnp.float32), jnp.zeros((width,), jnp.float32))
    entering = carried_in(
        (whole_filter, local_filter[steps_dev - 1]), "tm", compose, identity_pair, False
    )[1]
    filtered = local_filter + propagate(entering, closed, steps_dev)
    coupled = dot_high(smoother_gain, transition)
    global_rows = position * steps_dev + jnp.arange(steps_dev, dtype=jnp.int32)
    final_row = (global_rows == steps_dev * blocks - 1)[:, None]
    back = jnp.where(final_row, filtered, filtered - dot_high(filtered, coupled.T))
    local_smooth = block_prefix(back[::-1], smoother_gain)[::-1]
    whole_smooth = matrix_power(smoother_gain, steps_dev)
    arriving = carried_in((whole_smooth, local_smooth[0]), "tm", compose, identity_pair, True)[1]
    smoothed = local_smooth + propagate(arriving, smoother_gain, steps_dev)[::-1]
    factors_b = smoothed.astype(jnp.bfloat16)
    prior_row = shifted(smoothed[steps_dev - 1 :], "tm", 1)
    lag_rows = jnp.concatenate([prior_row, smoothed[: steps_dev - 1]], axis=0)
    kept_rows = jnp.where(final_row, 0.0, smoothed)
    total_part = dot_high(smoothed.T, smoothed)
    previous_part = dot_high(kept_rows.T, kept_rows)
    lagged_part = dot_high(smoothed.T, lag_rows)
    total, previous, lagged = lax.psum((total_part, previous_part, lagged_part), "tm")
    length = steps_dev * blocks
    total = total + length * smoothed_cov
    previous = previous + (length - 1) * smoothed_cov
    lagged = lagged + (length - 1) * dot_high(smoothed_cov, smoother_gain.T)
    window = observations
    cross = jnp.einsum(
        "ts,tk->sk",
        window,
        lax.all_gather(factors_b, "tm", axis=0, tiled=True),
        preferred_element_type=jnp.float32,
    )
    total_factor = jnp.linalg.cholesky(total)
    new_loadings = jax.scipy.linalg.cho_solve((total_factor, True), cross.T).T
    previous_factor = jnp.linalg.cholesky(previous)
    new_transition = jax.scipy.linalg.cho_solve((previous_factor, True), lagged.T).T
    return (smoothed, new_loadings, new_transition)


def solution(mesh):
    in_specs = (P(None, ("sr", "tm")), P(("sr", "tm"), None), P(("sr", "tm")), P(), P(), P(), P())
    out_specs = (P("tm", None), P(("sr", "tm"), None), P())
    return jax.shard_map(local, mesh=mesh, in_specs=in_specs, out_specs=out_specs, check_vma=False)
```

profile of v0, /device:TPU:0, one launch (start us, length us, event | category | flops | bytes accessed | tf_op | source)
XLA Modules:
  0.0 331.9 jit_solution(2547815003200978211)
XLA Ops:
  8.1 4.4 %fusion.13 = f32[128,128]{0,1:T(8,128)} fusion(f32[2048,128]{1,0:T(8,128)} %param.13, f32[2048]{0:T(1024)} %param.14), kind=kOutput, calls=%fused_computation.18 | convolution fusion | flops 402915328 | bytes 1122304 | tf_op jit(solution)/shard_map/dot_general | solution.py:32
  12.6 5.3 %convolution_bitcast_fusion.2 = f32[1024,128]{0,1:T(8,128)} fusion(bf16[1024,2048]{1,0:T(8,128)(2,1)} %param.12, f32[2048,128]{1,0:T(8,128)} %param.13, f32[2048]{0:T(1024)} %param.14), kind=kOutput, calls=%fused_computation.15 | convolution fusion | flops 537395200 | bytes 5775360 | tf_op jit(solution)/shard_map/dot_general | solution.py:88
  18.0 0.2 fusion.136
  18.6 0.3 convolution_multiply_fusion
  20.3 11.4 %all-gather.1 = f32[1024,128]{1,0:T(8,128)S(1)} all-gather(f32[128,128]{1,0:T(8,128)S(1)} %fusion.46), channel_id=3, replica_groups=mesh['tm'=8,'sr'=4] {'tm'}, dimensions={0}, use_global_device_ids=true | all-gather | bytes 589824 | tf_op jit(solution)/shard_map/all_gather | solution.py:13
  31.7 105.7 %all-reduce.21.cloned.1.call-done = f32[128,128]{0,1:T(8,128)} async-done(((f32[128,128]{0,1:T(8,128)}), f32[128,128]{0,1:T(8,128)}) %all-reduce.21.cloned.1.call-update) | async-done | bytes 65552 | tf_op jit(solution)/shard_map/psum | solution.py:95
  137.3 1.1 fusion.125
  138.5 0.3 fusion.16
  138.8 0.3 fusion.126
  140.6 10.4 %all-gather = f32[1024,128]{1,0:T(8,128)S(1)} all-gather(f32[128,128]{1,0:T(8,128)S(1)} %fusion.47), channel_id=2, replica_groups=mesh['tm'=8,'sr'=4] {'tm'}, dimensions={0}, use_global_device_ids=true | all-gather | bytes 589824 | tf_op jit(solution)/shard_map/all_gather | solution.py:13
  151.0 25.0 %all-reduce.19.cloned.1.call-done = f32[128,128]{0,1:T(8,128)} async-done(((f32[128,128]{0,1:T(8,128)}), f32[128,128]{0,1:T(8,128)}) %all-reduce.19.cloned.1.call-update) | async-done | bytes 65552 | tf_op jit(solution)/shard_map/psum | solution.py:94
  176.0 1.1 fusion.124
  177.3 0.3 convolution_add_fusion.12
  177.6 0.3 convolution_add_fusion.11
  177.8 0.3 convolution_add_fusion.10
  178.1 0.3 convolution_add_fusion.9
  178.4 0.3 convolution_add_fusion.8
  178.7 0.3 convolution_add_fusion.7
  179.0 8.8 %all-gather.2 = f32[8,1,128]{2,1,0:T(1,128)S(1)} all-gather(f32[1,1,128]{2,1,0:T(1,128)S(1)} %slice_bitcast_fusion.1), channel_id=1, replica_groups=mesh['tm'=8,'sr'=4] {'tm'}, dimensions={0}, use_global_device_ids=true | all-gather | bytes 4608 | tf_op jit(solution)/shard_map/all_gather | solution.py:13
  188.2 0.2 fusion.73
  188.5 0.2 fusion.57
  189.3 0.2 fusion.135
  189.5 0.3 fusion.12
  189.9 0.3 convolution_add_fusion.6
  190.1 0.3 convolution_add_fusion.5
  190.4 0.3 convolution_add_fusion.4
  190.7 0.3 convolution_add_fusion.3
  191.0 0.3 convolution_add_fusion.2
  191.3 0.3 convolution_add_fusion.1
  191.5 0.3 convolution_add_fusion
  191.8 9.7 %all-gather.3 = f32[8,1,128]{2,1,0:T(1,128)S(1)} all-gather(f32[1,1,128]{2,1,0:T(1,128)S(1)} %slice_bitcast_fusion), channel_id=1, replica_groups=mesh['tm'=8,'sr'=4] {'tm'}, dimensions={0}, use_global_device_ids=true | all-gather | bytes 4608 | tf_op jit(solution)/shard_map/all_gather | solution.py:13
  201.5 1.6 while.27
  201.7 0.2 fusion.247
  201.9 0.2 fusion.247
  202.2 0.2 fusion.247
  202.4 0.2 fusion.247
  202.6 0.2 fusion.247
  202.8 0.2 fusion.247
  203.1 0.2 fusion.95
  203.3 0.2 fusion.93
  203.5 0.2 fusion.89
  203.7 0.2 fusion.79
  204.0 0.2 fusion.65
  204.8 0.2 fusion.146
  205.1 1.0 fusion.36
  206.1 0.9 fusion.147
  207.0 2.0 collective-permute-start
  209.0 8.7 %all_gather.27 = bf16[1024,128]{1,0:T(8,128)(2,1)S(1)} all-gather(bf16[128,128]{1,0:T(8,128)(2,1)S(1)} %get-tuple-element.157), channel_id=1, replica_groups=mesh['tm'=8,'sr'=4] {'tm'}, dimensions={0}, use_global_device_ids=true | all-gather | bytes 294912 | tf_op jit(solution)/shard_map/all_gather | solution.py:129
  217.7 0.9 fusion.21
  218.7 2.9 fusion.148
  221.6 49.8 %all-reduce.23.cloned.1.call-done = (f32[128,128]{0,1:T(8,128)}, f32[128,128]{0,1:T(8,128)}, f32[128,128]{0,1:T(8,128)}) async-done(((f32[128,128]{0,1:T(8,128)}, f32[128,128]{0,1:T(8,128)}, f32[128,128]{0,1:T(8,128)}), (f32[128,128]{0,1:T(8,128)}, f32[128,128]{0,1:T(8,128)}, f32[128,128]{0,1:T(8,128)})) %all-reduce.23.cloned.1.call-update) | async-done | bytes 196624 | tf_op jit(solution)/shard_map/psum | solution.py:120
  271.4 0.9 multiply_add_fusion
  272.5 11.7 %cholesky.55 = f32[128,128]{1,0:T(8,128)S(1)} custom-call(f32[128,128]{1,0:T(8,128)S(1)} %get-tuple-element.161), custom_call_target="Cholesky" | custom-call | tf_op jit(solution)/shard_map/jit(cholesky)/cholesky | solution.py:134
  284.3 0.6 compare_reduce_fusion
  284.9 0.7 fusion.20
  285.6 9.8 %custom-call.17 = f32[1,128,128]{1,2,0:T(8,128)S(1)} custom-call(f32[1,128,128]{2,1,0:T(8,128)S(1)} %fusion.20), custom_call_target="InvertDiagBlocksLowerTriangular" | custom-call | tf_op jit(solution)/shard_map/jit(_cho_solve)/triangular_solve | solution.py:135
  295.4 1.1 fusion.27
  296.5 0.9 fusion.25
  297.4 11.7 %cholesky.44 = f32[128,128]{1,0:T(8,128)S(1)} custom-call(f32[128,128]{1,0:T(8,128)S(1)} %get-tuple-element.162), custom_call_target="Cholesky" | custom-call | tf_op jit(solution)/shard_map/jit(cholesky)/cholesky | solution.py:132
  309.2 0.6 compare_reduce_fusion.1
  309.8 0.7 fusion.19
  310.5 9.9 %custom-call.16 = f32[1,128,128]{1,2,0:T(8,128)S(1)} custom-call(f32[1,128,128]{2,1,0:T(8,128)S(1)} %fusion.19), custom_call_target="InvertDiagBlocksLowerTriangular" | custom-call | tf_op jit(solution)/shard_map/jit(_cho_solve)/triangular_solve | solution.py:133
  320.5 1.1 fusion.32
  321.5 2.8 fusion.30
  (87 shorter events, 6.0 us)
Async XLA Ops:
  8.0 10.0 %copy-start = (f32[128,128]{1,0:T(8,128)S(1)}, f32[128,128]{1,0:T(8,128)}, u32[]{:S(2)}) copy-start(f32[128,128]{1,0:T(8,128)} %param.17) | copy-start | bytes 196612
  8.0 9.9 %copy-start.2 = (f32[128,128]{1,0:T(8,128)S(1)}, f32[128,128]{1,0:T(8,128)}, u32[]{:S(2)}) copy-start(f32[128,128]{1,0:T(8,128)} %param.15) | copy-start | bytes 196612
  8.0 10.4 %copy-start.3 = (f32[128,128]{1,0:T(8,128)S(1)}, f32[128,128]{1,0:T(8,128)}, u32[]{:S(2)}) copy-start(f32[128,128]{1,0:T(8,128)} %param.18) | copy-start | bytes 196612
  8.0 129.3 %all-reduce.21.cloned.1.call-start = ((), (), s32[]{:S(2)}) async-start(), calls=%async_computation.3 | async-start | bytes 131072 | tf_op jit(solution)/shard_map/psum | solution.py:95
  12.5 126.0 %copy-start.4 = (f32[128,128]{1,0:T(8,128)S(1)}, f32[128,128]{1,0:T(8,128)}, u32[]{:S(2)}) copy-start(f32[128,128]{1,0:T(8,128)} %param.16) | copy-start | bytes 196612
  12.5 128.0 %reduce-scatter.2.cloned.1.call-start = ((), (), s32[]{:S(2)}) async-start(), calls=%async_computation.1 | async-start | bytes 589824 | tf_op jit(solution)/shard_map/reduce_scatter | solution.py:87
  17.9 158.1 %all-reduce.19.cloned.1.call-start = ((), (), s32[]{:S(2)}) async-start(), calls=%async_computation.2 | async-start | bytes 131072 | tf_op jit(solution)/shard_map/psum | solution.py:94
  140.6 130.9 %all-reduce.23.cloned.1.call-start = ((), (), s32[]{:S(2)}) async-start(), calls=%async_computation.4 | async-start | bytes 393216 | tf_op jit(solution)/shard_map/psum | solution.py:120
  205.1 105.4 %copy-start.1 = (f32[128,128]{1,0:T(8,128)}, f32[128,128]{1,0:T(8,128)S(1)}, u32[]{:S(2)}) copy-start(f32[128,128]{1,0:T(8,128)S(1)} %get-tuple-element.158) | copy-start | bytes 196612
  207.0 10.7 %collective-permute-start = (f32[1,128]{1,0:T(1,128)S(1)}, f32[1,128]{1,0:T(1,128)S(1)}, u32[]{:S(2)}, u32[]{:S(2)}) collective-permute-start(f32[1,128]{1,0:T(1,128)S(1)} %slice.121), channel_id=1, source_target_pairs={{0,4},{4,8},{8,12},{12,16},{16,20},{20,24},{24,28},{1,5},{5,9},{9,... | collective-permute-start | bytes 1544 | tf_op jit(solution)/shard_map/ppermute | solution.py:28
Sparse Core Ops, SparseCore 0:
  15.0 122.2 all-reduce.20
Sparse Core Ops, SparseCore 1:
  18.0 36.8 reduce-scatter.1
  140.6 35.2 all-reduce.18
  218.7 52.6 all-reduce.22
where the time goes:
time: 332 us
  waiting for transfers between devices  181 us (55%)
  blocking collectives  48.9 us (15%)
  other arithmetic  46.8 us (14%)
  matrix products  36.4 us (11%)
  between operations  16.2 us (5%)
    psum x1, waiting for transfers between devices, local(): info = lax.psum(info_part, ('tm', 'sr'))  106 us
    psum x1, waiting for transfers between devices, local(): lax.psum((total_part, previous_part, lagged_part), 'tm')  49.8 us
    all_gather x4, blocking collectives, carried_in(): gathered = jax.tree.map(lambda a: lax.all_gather(a, axis), part)  40.2 us
    psum x1, waiting for transfers between devices, local(): proj = lax.psum(partial_value, 'sr')  25 us
    dot_general x63, matrix products, dot_high(): jnp.dot(left, right, precision=precise, preferred_element_type=jnp.float32)  22.3 us
    another operation x3, other arithmetic, local(): previous_factor = jnp.linalg.cholesky(previous)  12.4 us
    another operation x3, other arithmetic, local(): total_factor = jnp.linalg.cholesky(total)  12.4 us
    another operation x2, other arithmetic, local(): new_loadings = jax.scipy.linalg.cho_solve((total_factor, True), cross.T).T  10.6 us
  transfers between devices with their start and end apart: 5, of which 3 were waited for; matrix products, arithmetic and copies ran while one was open for 4% of the time, Pallas kernels for 0%

commit v1 on v0

v1 whole, which is shorter than its diff:
```python
import functools
import jax
import jax.numpy as jnp
from jax import lax
from jax.experimental import pallas as pl
from jax.experimental.pallas import tpu as pltpu
from jax.sharding import PartitionSpec as P

precise = lax.Precision.HIGHEST
MESH = pl.DeviceIdType.MESH
SLABS = 8


def dot_high(left, right):
    return jnp.dot(left, right, precision=precise, preferred_element_type=jnp.float32)


def dot_first(left, right):
    return lax.dot_general(
        left, right, (((0,), (0,)), ((), ())), precision=precise, preferred_element_type=jnp.float32
    )


def halves(value):
    high = value.astype(jnp.bfloat16)
    low = (value - high.astype(jnp.float32)).astype(jnp.bfloat16)
    return high, low


def weights(matrix):
    high, low = halves(matrix)
    side = jnp.concatenate([high, low], axis=1)
    return jnp.concatenate([side, side], axis=0)


def times(value, doubled):
    high, low = halves(value)
    width = value.shape[1]
    out = jnp.dot(
        jnp.concatenate([high, low], axis=1), doubled, preferred_element_type=jnp.float32
    )
    return out[:, :width] + out[:, width:]


def reduce_kernel(
    chips, planes, part, out, pair_in, mine, chip_in, plane_in,
    pair_send, pair_recv, chip_send, chip_recv, plane_send, plane_recv,
    back_send, back_recv, last_send, last_recv,
):
    tm = lax.axis_index("tm")
    sr = lax.axis_index("sr")
    core = lax.rem(tm, 2)
    chip = tm // 2
    other = 1 - core
    partner = (2 * chip + other, sr)

    def chip_at(step):
        return lax.rem(chip + step, chips)

    def plane_at(step):
        return lax.rem(sr + step, planes)

    barrier = pltpu.get_barrier_semaphore()
    pl.semaphore_signal(barrier, inc=1, device_id=partner, device_id_type=MESH)
    for step in range(1, chips):
        pl.semaphore_signal(
            barrier, inc=1, device_id=(2 * chip_at(step) + core, sr), device_id_type=MESH
        )
    for step in range(1, planes):
        pl.semaphore_signal(barrier, inc=1, device_id=(tm, plane_at(step)), device_id_type=MESH)
    pl.semaphore_wait(barrier, 1 + chips - 1 + planes - 1)

    order = list(range(1, chips)) + [0]
    pairs = {}
    for step in order:
        target = chip_at(step)
        pairs[step] = pltpu.make_async_remote_copy(
            src_ref=part.at[other, target],
            dst_ref=pair_in.at[step],
            send_sem=pair_send.at[step],
            recv_sem=pair_recv.at[step],
            device_id=partner,
            device_id_type=MESH,
        )
        pairs[step].start()
    across = {}
    for step in order:
        pairs[step].wait_recv()
        mine[step] = part[core, chip_at(step)] + pair_in[step]
        if step > 0:
            across[step] = pltpu.make_async_remote_copy(
                src_ref=mine.at[step],
                dst_ref=chip_in.at[step],
                send_sem=chip_send.at[step],
                recv_sem=chip_recv.at[step],
                device_id=(2 * chip_at(step) + core, sr),
                device_id_type=MESH,
            )
            across[step].start()
    total = mine[0]
    for step in range(1, chips):
        across[step].wait_recv()
        total = total + chip_in[step]
    plane_in[sr] = total
    along = {}
    for step in range(1, planes):
        along[step] = pltpu.make_async_remote_copy(
            src_ref=plane_in.at[sr],
            dst_ref=plane_in.at[sr],
            send_sem=plane_send.at[step],
            recv_sem=plane_recv.at[step],
            device_id=(tm, plane_at(step)),
            device_id_type=MESH,
        )
        along[step].start()
    for step in range(1, planes):
        along[step].wait_recv()
    whole = plane_in[0]
    for plane in range(1, planes):
        whole = whole + plane_in[plane]
    out[core, chip] = whole
    back = {}
    for step in range(1, chips):
        back[step] = pltpu.make_async_remote_copy(
            src_ref=out.at[core, chip],
            dst_ref=out.at[core, chip],
            send_sem=back_send.at[step],
            recv_sem=back_recv.at[step],
            device_id=(2 * chip_at(step) + core, sr),
            device_id_type=MESH,
        )
        back[step].start()
    last = {}
    for step in range(chips):
        source = lax.rem(chip - step + chips, chips)
        if step > 0:
            back[step].wait_recv()
        last[step] = pltpu.make_async_remote_copy(
            src_ref=out.at[core, source],
            dst_ref=out.at[core, source],
            send_sem=last_send.at[step],
            recv_sem=last_recv.at[step],
            device_id=partner,
            device_id_type=MESH,
        )
        last[step].start()
    for step in range(chips):
        last[step].wait_recv()
    for copies in (pairs, across, along, back, last):
        for copy in copies.values():
            copy.wait_send()


def all_sum(part, planes):
    _, chips, rows, width = part.shape
    dma = pltpu.SemaphoreType.DMA
    vmem = pl.BlockSpec(memory_space=pltpu.VMEM)
    return pl.pallas_call(
        functools.partial(reduce_kernel, chips, planes),
        out_shape=jax.ShapeDtypeStruct(part.shape, jnp.float32),
        in_specs=[vmem],
        out_specs=vmem,
        scratch_shapes=[
            pltpu.VMEM((chips, rows, width), jnp.float32),
            pltpu.VMEM((chips, rows, width), jnp.float32),
            pltpu.VMEM((chips, rows, width), jnp.float32),
            pltpu.VMEM((planes, rows, width), jnp.float32),
        ]
        + [dma((chips,)), dma((chips,)), dma((chips,)), dma((chips,)), dma((planes,)), dma((planes,))]
        + [dma((chips,)), dma((chips,)), dma((chips,)), dma((chips,))],
        compiler_params=pltpu.CompilerParams(collective_id=0, has_side_effects=True),
        name="all_sum",
    )(part)


def shift_rows(value, steps):
    length = value.shape[0]
    row = lax.broadcasted_iota(jnp.int32, value.shape, 0)
    moved = pltpu.roll(value, steps % length, 0)
    keep = row >= steps if steps > 0 else row < length + steps
    return jnp.where(keep, moved, 0.0)


def powers(matrix, count):
    low = [matrix]
    while len(low) < SLABS:
        low = low + [dot_high(low[-1], each) for each in low]
    high = []
    square = low[-1]
    for _ in range(count - 1):
        square = dot_high(square, square)
        high.append(square)
    return [weights(each) for each in low], [weights(low[-1])] + [weights(each) for each in high]


def scan_slabs(slabs, low, high, reverse):
    order = list(range(SLABS))[::-1] if reverse else list(range(SLABS))
    sign = -1 if reverse else 1
    part = {order[0]: slabs[order[0]]}
    for before, now in zip(order, order[1:]):
        part[now] = slabs[now] + times(part[before], low[0])
    ends = part[order[-1]]
    for level, power in enumerate(high):
        ends = ends + times(shift_rows(ends, sign * 2**level), power)
    carry = shift_rows(ends, sign)
    out = [None] * SLABS
    for place, now in enumerate(order[:-1]):
        out[now] = part[now] + times(carry, low[place])
    out[order[-1]] = ends
    return out


def invert(matrices):
    size = matrices[0].shape[0]
    row_at = lax.broadcasted_iota(jnp.int32, (size, size), 0)
    lane_at = lax.broadcasted_iota(jnp.int32, (size, size), 1)
    lane = lax.broadcasted_iota(jnp.int32, (1, size), 1)
    for k in range(size):
        following = []
        for m in matrices:
            column = m[:, k : k + 1]
            row = m[k : k + 1, :]
            scale = 1.0 / m[k : k + 1, k : k + 1]
            row = jnp.where(lane == k, scale, row * scale)
            base = jnp.where(lane_at == k, 0.0, m)
            m = jnp.where(row_at == k, row, base - column * row)
            following.append(m)
        matrices = following
    return matrices


def smooth_kernel(
    length, total_in, transition, filter_cov, gain, cov, smoothed, inverse, moved, drive
):
    width = transition.shape[0]
    _, chips, rows, _ = total_in.shape
    block = length // (2 * chips)
    count = length // SLABS
    levels = (count - 1).bit_length()
    info = jnp.concatenate(
        [total_in[core, chip, block:, :] for chip in range(chips) for core in range(2)], axis=0
    )
    closed = transition[...] - dot_high(filter_cov[...], dot_high(info, transition[...]))
    low, high = powers(closed.T, levels)
    cov_t = weights(filter_cov[...].T)
    for chip in range(chips):
        for core in range(2):
            start = (2 * chip + core) * block
            drive[start : start + block, :] = times(total_in[core, chip, :block, :], cov_t)
    slabs = [drive[pl.ds(at, count, stride=SLABS), :] for at in range(SLABS)]
    filtered = scan_slabs(slabs, low, high, False)
    coupled = weights(dot_high(gain[...], transition[...]).T)
    last = lax.broadcasted_iota(jnp.int32, (count, width), 0) == count - 1
    back = [each - times(each, coupled) for each in filtered]
    back[-1] = jnp.where(last, filtered[-1], back[-1])
    low, high = powers(gain[...].T, levels)
    smooth = scan_slabs(back, low, high, True)
    for at in range(SLABS):
        smoothed[pl.ds(at, count, stride=SLABS), :] = smooth[at]
    kept = smooth[:-1] + [jnp.where(last, 0.0, smooth[-1])]
    previous = sum(dot_first(each, each) for each in kept)
    final = smooth[-1][count - 8 :, :]
    final = jnp.where(lax.broadcasted_iota(jnp.int32, final.shape, 0) == 7, final, 0.0)
    total = previous + dot_first(final, final)
    lag = [shift_rows(smooth[-1], 1)] + smooth[:-1]
    lagged = sum(dot_first(each, before) for each, before in zip(smooth, lag))
    total = total + length * cov[...]
    previous = previous + (length - 1) * cov[...]
    lagged = lagged + (length - 1) * dot_high(cov[...], gain[...].T)
    total, previous = invert([total, previous])
    inverse[...] = total
    moved[...] = dot_high(lagged, previous)


def local(
    observations, loadings, noise_precision, transition, filter_cov, smoother_gain, smoothed_cov
):
    blocks = lax.axis_size("tm")
    planes = lax.axis_size("sr")
    position = lax.axis_index("tm")
    width = transition.shape[0]
    length = observations.shape[0]
    steps_dev = length // blocks
    weighted = noise_precision[:, None] * loadings
    proj = jnp.dot(
        observations, weighted.astype(jnp.bfloat16), preferred_element_type=jnp.float32
    )
    info = dot_high(loadings.T, weighted)
    part = jnp.concatenate(
        [proj.reshape(blocks, steps_dev, width), info.reshape(blocks, width // blocks, width)], axis=1
    )
    part = part.reshape(blocks // 2, 2, part.shape[1], width).transpose(1, 0, 2, 3)
    summed = all_sum(part, planes)
    vmem = pl.BlockSpec(memory_space=pltpu.VMEM)
    smoothed, inverse, new_transition = pl.pallas_call(
        functools.partial(smooth_kernel, length),
        out_shape=[
            jax.ShapeDtypeStruct((length, width), jnp.float32),
            jax.ShapeDtypeStruct((width, width), jnp.float32),
            jax.ShapeDtypeStruct((width, width), jnp.float32),
        ],
        in_specs=[vmem] * 5,
        out_specs=[vmem] * 3,
        scratch_shapes=[pltpu.VMEM((length, width), jnp.float32)],
        name="smooth",
    )(summed, transition, filter_cov, smoother_gain, smoothed_cov)
    cross = jnp.einsum(
        "ts,tk->sk",
        observations,
        smoothed.astype(jnp.bfloat16),
        preferred_element_type=jnp.float32,
    )
    new_loadings = dot_high(cross, inverse)
    own = lax.dynamic_slice_in_dim(smoothed, position * steps_dev, steps_dev, 0)
    return (own, new_loadings, new_transition)


def solution(mesh):
    in_specs = (P(None, ("sr", "tm")), P(("sr", "tm"), None), P(("sr", "tm")), P(), P(), P(), P())
    out_specs = (P("tm", None), P(("sr", "tm"), None), P())
    return jax.shard_map(local, mesh=mesh, in_specs=in_specs, out_specs=out_specs, check_vma=False)
```

time: 332 us -> 69.4 us (0.21)
  waiting for transfers between devices: 181 us -> 0 us
  Pallas kernels: 0 us -> 51.8 us
  blocking collectives: 48.9 us -> 0 us
  other arithmetic: 46.8 us -> 0.86 us
  matrix products: 36.4 us -> 14 us
  between operations: 16.2 us -> 0.68 us
    psum x3 -> x0, waiting for transfers between devices: 180 us -> none  [the longest x1 106 us: local(): info = lax.psum(info_part, ('tm', 'sr'))]
    pallas_call x0 -> x2, Pallas kernels: none -> 51.8 us  [the longest x1 26.3 us: all_sum(): pl.pallas_call(functools.partial(reduce_kernel, chips, planes), out_shape...]
    all_gather x5 -> x0, blocking collectives: 48.9 us -> none  [the longest x4 40.2 us: carried_in(): gathered = jax.tree.map(lambda a: lax.all_gather(a, axis), part)]
    another operation x10 -> x0, other arithmetic: 45.8 us -> none  [the longest x3 12.4 us: local(): previous_factor = jnp.linalg.cholesky(previous)]
    dot_general x63 -> x2, matrix products: 22.3 us -> 6.47 us  [dot_high(): jnp.dot(left, right, precision=precise, preferred_element_type=jnp.float32)]
    another operation x4 -> x0, matrix products: 5.87 us -> none  [the longest x2 3.83 us: local(): new_loadings = jax.scipy.linalg.cho_solve((total_factor, True), cross.T).T]
  transfers between devices with their start and end apart: 5 -> 0, of which waited for: 3 -> 0; matrix products, arithmetic and copies ran while one was open for 4% -> 0% of each run, Pallas kernels for 0% -> 0%
where the time goes in v1:
time: 69.4 us; the launch traced here: 69.1 us
  Pallas kernels  51.8 us (75%)
  matrix products  14 us (20%)
  local copies, waits for them, and re-layouts  1.7 us (2%)
  other arithmetic  0.86 us (1%)
    pallas_call x1, Pallas kernels, all_sum(): pl.pallas_call(functools.partial(reduce_kernel, chips, planes), out_shape...  26.3 us
    pallas_call x1, Pallas kernels, local(): pl.pallas_call(functools.partial(smooth_kernel, length), out_shape=[jax.S...  25.5 us
    dot_general x2, matrix products, dot_high(): jnp.dot(left, right, precision=precise, preferred_element_type=jnp.float32)  6.47 us
    dot_general x1, matrix products, local(): jnp.dot(observations, weighted.astype(jnp.bfloat16), preferred_element_ty...  4.48 us
    dot_general x1, matrix products, local(): jnp.einsum('ts,tk->sk', observations, smoothed.astype(jnp.bfloat16), pref...  3.09 us
    dynamic_slice x1, local copies, waits for them, and re-layouts, local(): own = lax.dynamic_slice_in_dim(smoothed, position * steps_dev, steps_dev, 0)  1.5 us

profile of v1, /device:TPU:0, one launch (start us, length us, event | category | flops | bytes accessed | tf_op | source)
XLA Modules:
  0.0 69.1 jit_solution(13017350298183704991)
XLA Ops:
  0.6 3.7 %fusion = f32[128,128]{0,1:T(8,128)S(1)} fusion(f32[2048,128]{1,0:T(8,128)} %param.8, f32[2048]{0:T(1024)} %param.9), kind=kOutput, calls=%fused_computation | convolution fusion | flops 402915328 | bytes 1122304 | tf_op jit(solution)/shard_map/dot_general | solution.py:15
  4.3 4.5 %convolution_bitcast_fusion = f32[1024,128]{0,1:T(8,128)S(1)} fusion(bf16[1024,2048]{1,0:T(8,128)(2,1)} %param.7, f32[2048,128]{1,0:T(8,128)} %param.8, f32[2048]{0:T(1024)} %param.9), kind=kOutput, calls=%fused_computation.3 | convolution fusion | flops 537395200 | bytes 5775360 | tf_op jit(solution)/shard_map/dot_general | solution.py:285
  8.8 0.2 copy.10
  9.0 0.9 %copy_bitcast_fusion.part = f32[2,4,144,128]{3,2,1,0:T(8,128)} fusion(f32[4,2,16,128]{3,2,1,0:T(8,128)S(1)} %bitcast.14, f32[4,2,128,128]{3,2,1,0:T(8,128)S(1)} %bitcast.13), kind=kLoop, calls=%fused_computation.5 | loop fusion | flops 147456 | bytes 1179648 | tf_op jit(solution)/shard_map/transpose | solution.py:292
  9.9 26.3 %all_sum.1.total_in = f32[2,4,144,128]{3,2,1,0:T(8,128)} custom-call(f32[2,4,144,128]{3,2,1,0:T(8,128)} %copy_bitcast_fusion.part), custom_call_target="tpu_custom_call" | custom-call | tf_op jit(solution)/shard_map/all_sum/pallas_call | solution.py:158
  36.2 25.5 %smooth.1 = (f32[1024,128]{1,0:T(8,128)}, f32[128,128]{1,0:T(8,128)}, f32[128,128]{1,0:T(8,128)}) custom-call(f32[2,4,144,128]{3,2,1,0:T(8,128)} %all_sum.1.total_in, f32[128,128]{1,0:T(8,128)} %transition.1, f32[128,128]{1,0:T(8,128)} %filter_cov.1, f32[128,128]{1,0:T(8,128)} %gain.1, f32[128,128]{1,0:T(8,128)} %cov.1), custom_call_target="tpu_custom_call" | custom-call | tf_op jit(solution)/shard_map/smooth/pallas_call | solution.py:295
  61.7 0.0 copy-start
  61.7 1.5 %constant_dynamic-slice_fusion = f32[128,128]{1,0:T(8,128)} fusion(f32[1024,128]{1,0:T(8,128)} %get-tuple-element.6, s32[]{:T(128)S(6)} %select_n.3), kind=kLoop, calls=%fused_computation.10 | loop fusion | bytes 131076 | tf_op jit(solution)/shard_map/dynamic_slice | solution.py:314
  63.2 3.1 %fusion.4 = f32[128,2048]{1,0:T(8,128)S(1)} fusion(bf16[1024,2048]{1,0:T(8,128)(2,1)} %param.7, f32[1024,128]{1,0:T(8,128)} %get-tuple-element.6), kind=kOutput, calls=%fused_computation.8 | convolution fusion | flops 537001984 | bytes 5767168 | tf_op jit(solution)/shard_map/ts,tk->sk/dot_general | solution.py:307
  66.3 0.0 copy-done
  66.3 2.8 %fusion.6 = f32[2048,128]{1,0:T(8,128)} fusion(f32[128,2048]{1,0:T(8,128)S(1)} %fusion.4, f32[128,128]{1,0:T(8,128)S(1)} %copy-done), kind=kOutput, calls=%fused_computation.11 | convolution fusion | flops 402653184 | bytes 2162688 | tf_op jit(solution)/shard_map/dot_general | solution.py:15
Async XLA Ops:
  61.7 4.6 %copy-start = (f32[128,128]{1,0:T(8,128)S(1)}, f32[128,128]{1,0:T(8,128)}, u32[]{:S(2)}) copy-start(f32[128,128]{1,0:T(8,128)} %get-tuple-element.7) | copy-start | bytes 196612

commit v2 on v1

--- a/solution.py
+++ b/solution.py
@@ -9,6 +9,8 @@
 precise = lax.Precision.HIGHEST
 MESH = pl.DeviceIdType.MESH
 SLABS = 8
+PIECES = 2
+PIVOTS = 4
 
 
 def dot_high(left, right):
@@ -42,8 +44,60 @@
     return out[:, :width] + out[:, width:]
 
 
+def project_kernel(observations, loadings, precision, out):
+    _, chips, rows, width = out.shape
+    block = observations.shape[0] // (2 * chips)
+    depth = loadings.shape[0]
+    columns = [
+        jnp.broadcast_to(precision[pl.ds(at, 1), :], (width, width)).T
+        for at in range(depth // width)
+    ]
+    weighted = loadings[...] * jnp.concatenate(columns, axis=0)
+    proj = jnp.dot(
+        observations[...], weighted.astype(jnp.bfloat16), preferred_element_type=jnp.float32
+    )
+    left = jnp.concatenate(halves(loadings[...]), axis=1)
+    right = jnp.concatenate(halves(weighted), axis=1)
+    both = lax.dot_general(
+        left, right, (((0,), (0,)), ((), ())), preferred_element_type=jnp.float32
+    )
+    both = both[:width] + both[width:]
+    info = both[:, :width] + both[:, width:]
+    share = width // (2 * chips)
+
+    @pl.when(pl.program_id(0) == 0)
+    def _():
+        out[...] = jnp.zeros_like(out)
+
+    for chip in range(chips):
+        for core in range(2):
+            at = 2 * chip + core
+            out[core, chip, :block, :] += proj[at * block : (at + 1) * block]
+            out[core, chip, block:, :] += info[at * share : (at + 1) * share]
+
+
+def project(observations, loadings, noise_precision, blocks):
+    length, series = observations.shape
+    width = loadings.shape[1]
+    depth = min(series, 512)
+    lanes = depth // width
+    shape = (2, blocks // 2, (length + width) // blocks, width)
+    return pl.pallas_call(
+        project_kernel,
+        grid=(series // depth,),
+        out_shape=jax.ShapeDtypeStruct(shape, jnp.float32),
+        in_specs=[
+            pl.BlockSpec((length, depth), lambda at: (0, at)),
+            pl.BlockSpec((depth, width), lambda at: (at, 0)),
+            pl.BlockSpec((None, lanes, width), lambda at: (at, 0, 0)),
+        ],
+        out_specs=pl.BlockSpec(shape, lambda at: (0, 0, 0, 0)),
+        name="project",
+    )(observations, loadings, noise_precision.reshape(series // depth, lanes, width))
+
+
 def reduce_kernel(
-    chips, planes, part, out, pair_in, mine, chip_in, plane_in,
+    chips, planes, pieces, part, out, pair_in, mine, chip_in, plane_in,
     pair_send, pair_recv, chip_send, chip_recv, plane_send, plane_recv,
     back_send, back_recv, last_send, last_recv,
 ):
@@ -71,81 +125,86 @@
     pl.semaphore_wait(barrier, 1 + chips - 1 + planes - 1)
 
     order = list(range(1, chips)) + [0]
-    pairs = {}
-    for step in order:
-        target = chip_at(step)
-        pairs[step] = pltpu.make_async_remote_copy(
-            src_ref=part.at[other, target],
-            dst_ref=pair_in.at[step],
-            send_sem=pair_send.at[step],
-            recv_sem=pair_recv.at[step],
+    pairs, across, along, back, last = {}, {}, {}, {}, {}
+    for at, rows in enumerate(pieces):
+        for step in order:
+            target = chip_at(step)
+            pairs[at, step] = pltpu.make_async_remote_copy(
+                src_ref=part.at[other, target, rows],
+                dst_ref=pair_in.at[step, rows],
+                send_sem=pair_send.at[at, step],
+                recv_sem=pair_recv.at[at, step],
+                device_id=partner,
+                device_id_type=MESH,
+            )
+            pairs[at, step].start()
+    for at, rows in enumerate(pieces):
+        for step in order:
+            pairs[at, step].wait_recv()
+            mine[step, rows] = part[core, chip_at(step), rows] + pair_in[step, rows]
+            if step > 0:
+                across[at, step] = pltpu.make_async_remote_copy(
+                    src_ref=mine.at[step, rows],
+                    dst_ref=chip_in.at[step, rows],
+                    send_sem=chip_send.at[at, step],
+                    recv_sem=chip_recv.at[at, step],
+                    device_id=(2 * chip_at(step) + core, sr),
+                    device_id_type=MESH,
+                )
+                across[at, step].start()
+    for at, rows in enumerate(pieces):
+        total = mine[0, rows]
+        for step in range(1, chips):
+            across[at, step].wait_recv()
+            total = total + chip_in[step, rows]
+        plane_in[sr, rows] = total
+        for step in range(1, planes):
+            along[at, step] = pltpu.make_async_remote_copy(
+                src_ref=plane_in.at[sr, rows],
+                dst_ref=plane_in.at[sr, rows],
+                send_sem=plane_send.at[at, step],
+                recv_sem=plane_recv.at[at, step],
+                device_id=(tm, plane_at(step)),
+                device_id_type=MESH,
+            )
+            along[at, step].start()
+
+    def pass_on(at, rows, step):
+        source = lax.rem(chip - step + chips, chips)
+        last[at, step] = pltpu.make_async_remote_copy(
+            src_ref=out.at[core, source, rows],
+            dst_ref=out.at[core, source, rows],
+            send_sem=last_send.at[at, step],
+            recv_sem=last_recv.at[at, step],
             device_id=partner,
             device_id_type=MESH,
         )
-        pairs[step].start()
-    across = {}
-    for step in order:
-        pairs[step].wait_recv()
-        mine[step] = part[core, chip_at(step)] + pair_in[step]
-        if step > 0:
-            across[step] = pltpu.make_async_remote_copy(
-                src_ref=mine.at[step],
-                dst_ref=chip_in.at[step],
-                send_sem=chip_send.at[step],
-                recv_sem=chip_recv.at[step],
+        last[at, step].start()
+
+    for at, rows in enumerate(pieces):
+        for step in range(1, planes):
+            along[at, step].wait_recv()
+        whole = plane_in[0, rows]
+        for plane in range(1, planes):
+            whole = whole + plane_in[plane, rows]
+        out[core, chip, rows] = whole
+        for step in range(1, chips):
+            back[at, step] = pltpu.make_async_remote_copy(
+                src_ref=out.at[core, chip, rows],
+                dst_ref=out.at[core, chip, rows],
+                send_sem=back_send.at[at, step],
+                recv_sem=back_recv.at[at, step],
                 device_id=(2 * chip_at(step) + core, sr),
                 device_id_type=MESH,
             )
-            across[step].start()
-    total = mine[0]
-    for step in range(1, chips):
-        across[step].wait_recv()
-        total = total + chip_in[step]
-    plane_in[sr] = total
-    along = {}
-    for step in range(1, planes):
-        along[step] = pltpu.make_async_remote_copy(
-            src_ref=plane_in.at[sr],
-            dst_ref=plane_in.at[sr],
-            send_sem=plane_send.at[step],
-            recv_sem=plane_recv.at[step],
-            device_id=(tm, plane_at(step)),
-            device_id_type=MESH,
-        )
-        along[step].start()
-    for step in range(1, planes):
-        along[step].wait_recv()
-    whole = plane_in[0]
-    for plane in range(1, planes):
-        whole = whole + plane_in[plane]
-    out[core, chip] = whole
-    back = {}
-    for step in range(1, chips):
-        back[step] = pltpu.make_async_remote_copy(
-            src_ref=out.at[core, chip],
-            dst_ref=out.at[core, chip],
-            send_sem=back_send.at[step],
-            recv_sem=back_recv.at[step],
-            device_id=(2 * chip_at(step) + core, sr),
-            device_id_type=MESH,
-        )
-        back[step].start()
-    last = {}
-    for step in range(chips):
-        source = lax.rem(chip - step + chips, chips)
-        if step > 0:
-            back[step].wait_recv()
-        last[step] = pltpu.make_async_remote_copy(
-            src_ref=out.at[core, source],
-            dst_ref=out.at[core, source],
-            send_sem=last_send.at[step],
-            recv_sem=last_recv.at[step],
-            device_id=partner,
-            device_id_type=MESH,
-        )
-        last[step].start()
-    for step in range(chips):
-        last[step].wait_recv()
+            back[at, step].start()
+        pass_on(at, rows, 0)
+    for at, rows in enumerate(pieces):
+        for step in range(1, chips):
+            back[at, step].wait_recv()
+            pass_on(at, rows, step)
+    for copy in last.values():
+        copy.wait_recv()
     for copies in (pairs, across, along, back, last):
         for copy in copies.values():
             copy.wait_send()
@@ -154,9 +213,11 @@
 def all_sum(part, planes):
     _, chips, rows, width = part.shape
     dma = pltpu.SemaphoreType.DMA
+    cuts = [rows * at // PIECES // 8 * 8 for at in range(PIECES)] + [rows]
+    pieces = [slice(start, stop) for start, stop in zip(cuts, cuts[1:])]
     vmem = pl.BlockSpec(memory_space=pltpu.VMEM)
     return pl.pallas_call(
-        functools.partial(reduce_kernel, chips, planes),
+        functools.partial(reduce_kernel, chips, planes, pieces),
         out_shape=jax.ShapeDtypeStruct(part.shape, jnp.float32),
         in_specs=[vmem],
         out_specs=vmem,
@@ -166,8 +227,9 @@
             pltpu.VMEM((chips, rows, width), jnp.float32),
             pltpu.VMEM((planes, rows, width), jnp.float32),
         ]
-        + [dma((chips,)), dma((chips,)), dma((chips,)), dma((chips,)), dma((planes,)), dma((planes,))]
-        + [dma((chips,)), dma((chips,)), dma((chips,)), dma((chips,))],
+        + [dma((PIECES, chips))] * 4
+        + [dma((PIECES, planes))] * 2
+        + [dma((PIECES, chips))] * 4,
         compiler_params=pltpu.CompilerParams(collective_id=0, has_side_effects=True),
         name="all_sum",
     )(part)
@@ -210,23 +272,88 @@
     return out
 
 
+def inverse_two(a, b, c):
+    scale = 1.0 / (a * c - b * b)
+    return c * scale, -b * scale, a * scale
+
+
+def inverse_four(p):
+    e, f, g = inverse_two(p[0][0], p[0][1], p[1][1])
+    u00 = e * p[0][2] + f * p[1][2]
+    u01 = e * p[0][3] + f * p[1][3]
+    u10 = f * p[0][2] + g * p[1][2]
+    u11 = f * p[0][3] + g * p[1][3]
+    s00 = p[2][2] - (p[0][2] * u00 + p[1][2] * u10)
+    s01 = p[2][3] - (p[0][2] * u01 + p[1][2] * u11)
+    s11 = p[3][3] - (p[0][3] * u01 + p[1][3] * u11)
+    t00, t01, t11 = inverse_two(s00, s01, s11)
+    v00 = u00 * t00 + u01 * t01
+    v01 = u00 * t01 + u01 * t11
+    v10 = u10 * t00 + u11 * t01
+    v11 = u10 * t01 + u11 * t11
+    a00 = e + (v00 * u00 + v01 * u01)
+    a01 = f + (v00 * u10 + v01 * u11)
+    a11 = g + (v10 * u10 + v11 * u11)
+    return [
+        [a00, a01, -v00, -v01],
+        [a01, a11, -v10, -v11],
+        [-v00, -v10, t00, t01],
+        [-v01, -v11, t01, t11],
+    ]
+
+
 def invert(matrices):
     size = matrices[0].shape[0]
     row_at = lax.broadcasted_iota(jnp.int32, (size, size), 0)
     lane_at = lax.broadcasted_iota(jnp.int32, (size, size), 1)
-    lane = lax.broadcasted_iota(jnp.int32, (1, size), 1)
-    for k in range(size):
+    lane = lax.broadcasted_iota(jnp.int32, (8, size), 1)
+    diagonal = row_at == lane_at
+    scales, scaled = [], []
+    for m in matrices:
+        only = jnp.where(diagonal, m, 0.0)
+        across = lax.rsqrt(jnp.sum(only, axis=0, keepdims=True))
+        down = lax.rsqrt(jnp.sum(only, axis=1, keepdims=True))
+        scales.append((across, down))
+        scaled.append((m * across) * down)
+    matrices = scaled
+    for k in range(0, size, PIVOTS):
         following = []
+        group = k // 8 * 8
         for m in matrices:
-            column = m[:, k : k + 1]
-            row = m[k : k + 1, :]
-            scale = 1.0 / m[k : k + 1, k : k + 1]
-            row = jnp.where(lane == k, scale, row * scale)
-            base = jnp.where(lane_at == k, 0.0, m)
-            m = jnp.where(row_at == k, row, base - column * row)
-            following.append(m)
+            columns = [jnp.broadcast_to(m[:, k + j : k + j + 1], m.shape) for j in range(PIVOTS)]
+
+            def spread(value, at):
+                return jnp.broadcast_to(value[at : at + 1, :], (8, size))
+
+            block = [
+                [spread(columns[j], k + min(i, j)) if i <= j else None for j in range(PIVOTS)]
+                for i in range(PIVOTS)
+            ]
+            rows = [spread(m, k + i) for i in range(PIVOTS)]
+            solved = inverse_four(block)
+            fresh = []
+            for i in range(PIVOTS):
+                row = solved[i][0] * rows[0]
+                for j in range(1, PIVOTS):
+                    row = row + solved[i][j] * rows[j]
+                for j in range(PIVOTS):
+                    row = jnp.where(lane == k + j, solved[i][j], row)
+                fresh.append(row)
+            parts = []
+            for start in range(0, size, 8):
+                here = slice(start, start + 8)
+                value = jnp.where((lane >= k) & (lane < k + PIVOTS), 0.0, m[here])
+                take = columns[0][here] * fresh[0]
+                for i in range(1, PIVOTS):
+                    take = take + columns[i][here] * fresh[i]
+                value = value - take
+                if start == group:
+                    for i in range(PIVOTS):
+                        value = jnp.where(row_at[here] == k + i, fresh[i], value)
+                parts.append(value)
+            following.append(jnp.concatenate(parts, axis=0))
         matrices = following
-    return matrices
+    return [(m * across) * down for m, (across, down) in zip(matrices, scales)]
 
 
 def smooth_kernel(
@@ -281,15 +408,7 @@
     width = transition.shape[0]
     length = observations.shape[0]
     steps_dev = length // blocks
-    weighted = noise_precision[:, None] * loadings
-    proj = jnp.dot(
-        observations, weighted.astype(jnp.bfloat16), preferred_element_type=jnp.float32
-    )
-    info = dot_high(loadings.T, weighted)
-    part = jnp.concatenate(
-        [proj.reshape(blocks, steps_dev, width), info.reshape(blocks, width // blocks, width)], axis=1
-    )
-    part = part.reshape(blocks // 2, 2, part.shape[1], width).transpose(1, 0, 2, 3)
+    part = project(observations, loadings, noise_precision, blocks)
     summed = all_sum(part, planes)
     vmem = pl.BlockSpec(memory_space=pltpu.VMEM)
     smoothed, inverse, new_transition = pl.pallas_call(

time: 69.4 us -> 63 us (0.908)
  matrix products: 14 us -> 5.88 us
  Pallas kernels: 51.8 us -> 54.6 us
  other arithmetic: 0.86 us -> 0 us
    dot_general x1 -> x0, matrix products: 4.48 us -> none  [local(): jnp.dot(observations, weighted.astype(jnp.bfloat16), preferred_element_ty...]
    pallas_call x1 -> x2, Pallas kernels: 26.3 us -> 30.7 us  [the longest x1 25.1 us: all_sum(): pl.pallas_call(functools.partial(reduce_kernel, chips, planes, pieces), o...]
    dot_general x2 -> x1, matrix products: 6.47 us -> 2.79 us  [dot_high(): jnp.dot(left, right, precision=precise, preferred_element_type=jnp.float32)]
    pallas_call x1, Pallas kernels: 25.5 us -> 23.9 us  [local(): pl.pallas_call(functools.partial(smooth_kernel, length), out_shape=[jax.S...]
    transpose x1 -> x0, other arithmetic: 0.86 us -> none  [local(): part.reshape(blocks // 2, 2, part.shape[1], width).transpose(1, 0, 2, 3)]
where the time goes in v2:
time: 63 us; the launch traced here: 62.6 us
  Pallas kernels  54.6 us (87%)
  matrix products  5.88 us (9%)
  local copies, waits for them, and re-layouts  1.51 us (2%)
  between operations  0.66 us (1%)
    pallas_call x1, Pallas kernels, all_sum(): pl.pallas_call(functools.partial(reduce_kernel, chips, planes, pieces), o...  25.1 us
    pallas_call x1, Pallas kernels, local(): pl.pallas_call(functools.partial(smooth_kernel, length), out_shape=[jax.S...  23.9 us
    pallas_call x1, Pallas kernels, project(): pl.pallas_call(project_kernel, grid=(series // depth,), out_shape=jax.Sha...  5.55 us
    dot_general x1, matrix products, local(): jnp.einsum('ts,tk->sk', observations, smoothed.astype(jnp.bfloat16), pref...  3.1 us
    dot_general x1, matrix products, dot_high(): jnp.dot(left, right, precision=precise, preferred_element_type=jnp.float32)  2.79 us
    dynamic_slice x1, local copies, waits for them, and re-layouts, local(): own = lax.dynamic_slice_in_dim(smoothed, position * steps_dev, steps_dev, 0)  1.5 us

profile of v2, /device:TPU:0, one launch (start us, length us, event | category | flops | bytes accessed | tf_op | source)
XLA Modules:
  0.0 62.6 jit_solution(10807673355914264055)
XLA Ops:
  0.6 5.5 %project.1.part = f32[2,4,144,128]{3,2,1,0:T(8,128)} custom-call(bf16[1024,2048]{1,0:T(8,128)(2,1)} %observations.1, f32[2048,128]{1,0:T(8,128)} %loadings.1, f32[4,4,128]{2,1,0:T(4,128)} %bitcast.4), custom_call_target="tpu_custom_call" | custom-call | tf_op jit(solution)/shard_map/project/pallas_call | solution.py:85
  6.2 25.1 %all_sum.1.total_in = f32[2,4,144,128]{3,2,1,0:T(8,128)} custom-call(f32[2,4,144,128]{3,2,1,0:T(8,128)} %project.1.part), custom_call_target="tpu_custom_call" | custom-call | tf_op jit(solution)/shard_map/all_sum/pallas_call | solution.py:219
  31.3 23.9 %smooth.1 = (f32[1024,128]{1,0:T(8,128)}, f32[128,128]{1,0:T(8,128)}, f32[128,128]{1,0:T(8,128)}) custom-call(f32[2,4,144,128]{3,2,1,0:T(8,128)} %all_sum.1.total_in, f32[128,128]{1,0:T(8,128)} %transition.1, f32[128,128]{1,0:T(8,128)} %filter_cov.1, f32[128,128]{1,0:T(8,128)} %gain.1, f32[128,128]{1,0:T(8,128)} %cov.1), custom_call_target="tpu_custom_call" | custom-call | tf_op jit(solution)/shard_map/smooth/pallas_call | solution.py:414
  55.2 0.0 copy-start
  55.2 1.5 %constant_dynamic-slice_fusion = f32[128,128]{1,0:T(8,128)} fusion(f32[1024,128]{1,0:T(8,128)} %get-tuple-element.6, s32[]{:T(128)S(6)} %select_n.3), kind=kLoop, calls=%fused_computation.2 | loop fusion | bytes 131076 | tf_op jit(solution)/shard_map/dynamic_slice | solution.py:433
  56.7 3.1 %fusion = f32[128,2048]{1,0:T(8,128)S(1)} fusion(bf16[1024,2048]{1,0:T(8,128)(2,1)} %observations.1, f32[1024,128]{1,0:T(8,128)} %get-tuple-element.6), kind=kOutput, calls=%fused_computation | convolution fusion | flops 537001984 | bytes 5767168 | tf_op jit(solution)/shard_map/ts,tk->sk/dot_general | solution.py:426
  59.8 0.0 copy-done
  59.9 2.8 %fusion.2 = f32[2048,128]{1,0:T(8,128)} fusion(f32[128,2048]{1,0:T(8,128)S(1)} %fusion, f32[128,128]{1,0:T(8,128)S(1)} %copy-done), kind=kOutput, calls=%fused_computation.3 | convolution fusion | flops 402653184 | bytes 2162688 | tf_op jit(solution)/shard_map/dot_general | solution.py:17
Async XLA Ops:
  55.2 4.6 %copy-start = (f32[128,128]{1,0:T(8,128)S(1)}, f32[128,128]{1,0:T(8,128)}, u32[]{:S(2)}) copy-start(f32[128,128]{1,0:T(8,128)} %get-tuple-element.7) | copy-start | bytes 196612

commit v3 on v2

--- a/solution.py
+++ b/solution.py
@@ -357,8 +357,12 @@
 
 
 def smooth_kernel(
-    length, total_in, transition, filter_cov, gain, cov, smoothed, inverse, moved, drive
+    total_in, transition, filter_cov, gain, cov, observations, own, updated, moved,
+    drive, held, arrived,
 ):
+    length = observations.shape[0]
+    panel = pltpu.make_async_copy(observations, held, arrived)
+    panel.start()
     width = transition.shape[0]
     _, chips, rows, _ = total_in.shape
     block = length // (2 * chips)
@@ -383,7 +387,9 @@
     low, high = powers(gain[...].T, levels)
     smooth = scan_slabs(back, low, high, True)
     for at in range(SLABS):
-        smoothed[pl.ds(at, count, stride=SLABS), :] = smooth[at]
+        drive[pl.ds(at, count, stride=SLABS), :] = smooth[at]
+    place = pl.multiple_of(lax.axis_index("tm") * block, block)
+    own[...] = drive[pl.ds(place, block), :]
     kept = smooth[:-1] + [jnp.where(last, 0.0, smooth[-1])]
     previous = sum(dot_first(each, each) for each in kept)
     final = smooth[-1][count - 8 :, :]
@@ -394,8 +400,18 @@
     total = total + length * cov[...]
     previous = previous + (length - 1) * cov[...]
     lagged = lagged + (length - 1) * dot_high(cov[...], gain[...].T)
+    factors = drive[...].T.astype(jnp.bfloat16)
+    panel.wait()
+    series = updated.shape[0]
+    parts = [slice(start, min(start + 256, series)) for start in range(0, series, 256)]
+    for part in parts:
+        updated[part, :] = jnp.dot(
+            factors, held[:, part], preferred_element_type=jnp.float32
+        ).T
     total, previous = invert([total, previous])
-    inverse[...] = total
+    total = weights(total)
+    for part in parts:
+        updated[part, :] = times(updated[part, :], total)
     moved[...] = dot_high(lagged, previous)
 
 
@@ -404,34 +420,29 @@
 ):
     blocks = lax.axis_size("tm")
     planes = lax.axis_size("sr")
-    position = lax.axis_index("tm")
     width = transition.shape[0]
     length = observations.shape[0]
     steps_dev = length // blocks
     part = project(observations, loadings, noise_precision, blocks)
     summed = all_sum(part, planes)
     vmem = pl.BlockSpec(memory_space=pltpu.VMEM)
-    smoothed, inverse, new_transition = pl.pallas_call(
-        functools.partial(smooth_kernel, length),
+    series = observations.shape[1]
+    return pl.pallas_call(
+        smooth_kernel,
         out_shape=[
-            jax.ShapeDtypeStruct((length, width), jnp.float32),
-            jax.ShapeDtypeStruct((width, width), jnp.float32),
+            jax.ShapeDtypeStruct((steps_dev, width), jnp.float32),
+            jax.ShapeDtypeStruct((series, width), jnp.float32),
             jax.ShapeDtypeStruct((width, width), jnp.float32),
         ],
-        in_specs=[vmem] * 5,
+        in_specs=[vmem] * 5 + [pl.BlockSpec(memory_space=pl.ANY)],
         out_specs=[vmem] * 3,
-        scratch_shapes=[pltpu.VMEM((length, width), jnp.float32)],
+        scratch_shapes=[
+            pltpu.VMEM((length, width), jnp.float32),
+            pltpu.VMEM((length, series), observations.dtype),
+            pltpu.SemaphoreType.DMA,
+        ],
         name="smooth",
-    )(summed, transition, filter_cov, smoother_gain, smoothed_cov)
-    cross = jnp.einsum(
-        "ts,tk->sk",
-        observations,
-        smoothed.astype(jnp.bfloat16),
-        preferred_element_type=jnp.float32,
-    )
-    new_loadings = dot_high(cross, inverse)
-    own = lax.dynamic_slice_in_dim(smoothed, position * steps_dev, steps_dev, 0)
-    return (own, new_loadings, new_transition)
+    )(summed, transition, filter_cov, smoother_gain, smoothed_cov, observations)
 
 
 def solution(mesh):

time: 63 us -> 53.5 us (0.85)
  matrix products: 5.88 us -> 0 us
  Pallas kernels: 54.6 us -> 52.4 us
  local copies, waits for them, and re-layouts: 1.51 us -> 0 us
    dot_general x2 -> x0, matrix products: 5.88 us -> none  [the longest x1 3.1 us: local(): jnp.einsum('ts,tk->sk', observations, smoothed.astype(jnp.bfloat16), pref...]
    pallas_call x1, Pallas kernels: 23.9 us -> 21.8 us  [local(): pl.pallas_call(smooth_kernel, out_shape=[jax.ShapeDtypeStruct((steps_dev,...]
    dynamic_slice x1 -> x0, local copies, waits for them, and re-layouts: 1.5 us -> none  [local(): own = lax.dynamic_slice_in_dim(smoothed, position * steps_dev, steps_dev, 0)]
where the time goes in v3:
time: 53.5 us; the launch traced here: 53.2 us
  Pallas kernels  52.4 us (98%)
  between operations  0.8 us (1%)
    pallas_call x1, Pallas kernels, all_sum(): pl.pallas_call(functools.partial(reduce_kernel, chips, planes, pieces), o...  25.1 us
    pallas_call x1, Pallas kernels, local(): pl.pallas_call(smooth_kernel, out_shape=[jax.ShapeDtypeStruct((steps_dev,...  21.8 us
    pallas_call x1, Pallas kernels, project(): pl.pallas_call(project_kernel, grid=(series // depth,), out_shape=jax.Sha...  5.55 us

profile of v3, /device:TPU:0, one launch (start us, length us, event | category | flops | bytes accessed | tf_op | source)
XLA Modules:
  0.0 53.2 jit_solution(6535441535178301660)
XLA Ops:
  0.6 5.6 %project.1.part = f32[2,4,144,128]{3,2,1,0:T(8,128)} custom-call(bf16[1024,2048]{1,0:T(8,128)(2,1)} %observations.3, f32[2048,128]{1,0:T(8,128)} %loadings.1, f32[4,4,128]{2,1,0:T(4,128)} %bitcast.1), custom_call_target="tpu_custom_call" | custom-call | tf_op jit(solution)/shard_map/project/pallas_call | solution.py:85
  6.2 25.1 %all_sum.1.total_in = f32[2,4,144,128]{3,2,1,0:T(8,128)} custom-call(f32[2,4,144,128]{3,2,1,0:T(8,128)} %project.1.part), custom_call_target="tpu_custom_call" | custom-call | tf_op jit(solution)/shard_map/all_sum/pallas_call | solution.py:219
  31.3 21.8 %smooth.1 = (f32[128,128]{1,0:T(8,128)}, f32[2048,128]{1,0:T(8,128)}, f32[128,128]{1,0:T(8,128)}) custom-call(f32[2,4,144,128]{3,2,1,0:T(8,128)} %all_sum.1.total_in, f32[128,128]{1,0:T(8,128)} %transition.1, f32[128,128]{1,0:T(8,128)} %filter_cov.1, f32[128,128]{1,0:T(8,128)} %gain.1, f32[128,128]{1,0:T(8,128)} %cov.1, bf16[1024,2048]{1,0:T(8,128)(2,1)} %observations.3), custom_call_target="tpu_custom_call" | custom-call | tf_op jit(solution)/shard_map/smooth/pallas_call | solution.py:430
